TPU v7x, 8 devices: a whole 2x2x1 slice. The times are simulated.
8 devices in a mesh: dp: 1 (over z), tp: 8 (over x, y, core).
Axes of the slice: x: 2, y: 2, z: 1, core: 2. Of those that a mesh axis runs over, the one named last changes fastest.
Arguments:
- x: bfloat16 [2048, 2304], P('dp')
- dy: bfloat16 [2048, 2304], P('dp')
- gate: bfloat16 [2048, 9216], P('dp', 'tp')
- up: bfloat16 [2048, 9216], P('dp', 'tp')
- w_gate: bfloat16 [2304, 9216], P(None, 'tp')
- w_up: bfloat16 [2304, 9216], P(None, 'tp')
- w_down: bfloat16 [9216, 2304], P('tp')
Outputs:
- output 1: bfloat16 [2048, 2304], P('dp')
- output 2: bfloat16 [2304, 9216], P('dp', 'tp')
- output 3: bfloat16 [2304, 9216], P('dp', 'tp')
- output 4: bfloat16 [9216, 2304], P(('dp', 'tp'))
All inputs are finite; a program needn't handle non-finite values.
Results may differ from a plain program's by a relative error of at most 0.012.
Values are sent between devices in bfloat16 or wider.
A program may use at most 2 GiB of HBM per device.

v0:
```python
import jax
import jax.numpy as jnp
from jax import lax
from jax.sharding import PartitionSpec as P


def act(gate, up):
    return jax.nn.gelu(gate) * up


def solution(mesh):
    def step(x, dy, gate, up, w_gate, w_up, w_down):
        hidden, back = jax.vjp(act, gate.astype(jnp.float32), up.astype(jnp.float32))
        d_hidden = jnp.dot(dy, w_down.T, preferred_element_type=jnp.float32)
        d_gate, d_up = (g.astype(jnp.bfloat16) for g in back(d_hidden))
        term = jnp.dot(d_gate, w_gate.T, preferred_element_type=jnp.float32) + jnp.dot(d_up, w_up.T, preferred_element_type=jnp.float32)
        dx = lax.psum(term.astype(jnp.bfloat16), "tp")
        dw_gate = jnp.dot(x.T, d_gate, preferred_element_type=jnp.float32)
        dw_up = jnp.dot(x.T, d_up, preferred_element_type=jnp.float32)
        dw_down = jnp.dot(hidden.astype(jnp.bfloat16).T, dy, preferred_element_type=jnp.float32)
        return dx, *(g.astype(jnp.bfloat16) for g in (dw_gate, dw_up, dw_down))

    tokens, columns, rows = P("dp", None), P(None, "tp"), P("tp", None)
    return jax.shard_map(
        step,
        mesh=mesh,
        in_specs=(tokens, tokens, P("dp", "tp"), P("dp", "tp"), columns, columns, rows),
        out_specs=(tokens, P("dp", "tp"), P("dp", "tp"), P(("dp", "tp"), None)),
        check_vma=False,
    )
```

profile of v0, /device:TPU:0, one launch (start us, length us, event | category | flops | bytes accessed | tf_op | source)
XLA Modules:
  0.0 217.1 jit_solution(12265205882270599404)
XLA Ops:
  7.2 0.0 all-reduce.2.cloned.1.call-start
  7.2 0.0 copy-start
  7.2 26.2 %fusion.6 = (bf16[2048,1152]{1,0:T(8,128)(2,1)}, f32[2048,1152]{1,0:T(8,128)}) fusion(bf16[2048,1152]{1,0:T(8,128)(2,1)} %param.9, bf16[2048,1152]{1,0:T(8,128)(2,1)} %param.10, bf16[2048,2304]{1,0:T(8,128)(2,1)} %param.8, bf16[1152,2304]{1,0:T(8,128)(2,1)} %param.13), kind=kOutput, calls=%fused_computation.17 | convolution fusion | flops 10925899776 | bytes 38338560 | tf_op jit(solution)/shard_map/dot_general | solution.py:14
  33.4 0.0 copy-done
  33.4 16.9 %fusion.21 = f32[2048,2304]{1,0:T(8,128)} fusion(bf16[2048,1152]{1,0:T(8,128)(2,1)} %get-tuple-element.8, bf16[2304,1152]{1,0:T(8,128)(2,1)S(1)} %copy-done), kind=kOutput, calls=%fused_computation.32 | convolution fusion | flops 10871635968 | bytes 28901376 | tf_op jit(solution)/shard_map/dot_general | solution.py:16
  50.3 22.8 %add_convert_fusion = bf16[2048,2304]{1,0:T(8,128)(2,1)} fusion(f32[2048,2304]{1,0:T(8,128)} %fusion.21, bf16[2304,1152]{1,0:T(8,128)(2,1)} %param.12, f32[2048,1152]{1,0:T(8,128)} %get-tuple-element.9, bf16[2048,1152]{1,0:T(8,128)(2,1)} %param.9), kind=kOutput, calls=%fused_computation | convolution fusion | flops 10907025408 | bytes 47775744 | tf_op jit(solution)/shard_map/dot_general | solution.py:16
  73.2 0.0 all-reduce.2.cloned.1.call-update
  73.2 17.1 %fusion.1 = bf16[2304,1152]{0,1:T(8,128)(2,1)} fusion(bf16[2048,1152]{1,0:T(8,128)(2,1)} %get-tuple-element.8, bf16[2048,2304]{1,0:T(8,128)(2,1)} %param.7), kind=kOutput, calls=%fused_computation.12 | convolution fusion | flops 10874290176 | bytes 19464192 | tf_op jit(solution)/shard_map/dot_general | solution.py:18
  90.3 8.5 %copy.11 = bf16[2304,1152]{1,0:T(8,128)(2,1)} copy(bf16[2304,1152]{0,1:T(8,128)(2,1)} %fusion.1) | data formatting | bytes 10616832
  98.8 18.9 %fusion.2 = bf16[2304,1152]{0,1:T(8,128)(2,1)} fusion(bf16[2048,2304]{1,0:T(8,128)(2,1)} %param.7, f32[2048,1152]{1,0:T(8,128)} %get-tuple-element.9, bf16[2048,1152]{1,0:T(8,128)(2,1)} %param.9), kind=kOutput, calls=%fused_computation.13 | convolution fusion | flops 10900242432 | bytes 28901376 | tf_op jit(solution)/shard_map/dot_general | solution.py:19
  117.8 8.5 %copy.12 = bf16[2304,1152]{1,0:T(8,128)(2,1)} copy(bf16[2304,1152]{0,1:T(8,128)(2,1)} %fusion.2) | data formatting | bytes 10616832
  126.3 18.8 %convolution_convert_fusion = bf16[1152,2304]{1,0:T(8,128)(2,1)} fusion(bf16[2048,2304]{1,0:T(8,128)(2,1)} %param.8, bf16[2048,1152]{1,0:T(8,128)(2,1)} %param.10, bf16[2048,1152]{1,0:T(8,128)(2,1)} %param.9), kind=kOutput, calls=%fused_computation.9 | convolution fusion | flops 10902601728 | bytes 24182784 | tf_op jit(solution)/shard_map/dot_general | solution.py:20
  145.1 57.2 %all-reduce.2.cloned.1.call-done = bf16[2048,2304]{1,0:T(8,128)(2,1)} async-done(((bf16[2048,2304]{1,0:T(8,128)(2,1)}), bf16[2048,2304]{1,0:T(8,128)(2,1)}) %all-reduce.2.cloned.1.call-update) | async-done | bytes 9437200 | tf_op jit(solution)/shard_map/psum | solution.py:17
  202.3 8.0 %copy.14 = bf16[2048,2304]{1,0:T(8,128)(2,1)} copy(bf16[2048,2304]{1,0:T(8,128)(2,1)} %all-reduce.2.cloned.1.call-done) | data formatting | bytes 18874368
Async XLA Ops:
  7.2 195.1 %all-reduce.2.cloned.1.call-start = ((), (), s32[]{:S(2)}) async-start(), calls=%async_computation | async-start | bytes 18874368 | tf_op jit(solution)/shard_map/psum | solution.py:17
  7.2 26.2 %copy-start = (bf16[2304,1152]{1,0:T(8,128)(2,1)S(1)}, bf16[2304,1152]{1,0:T(8,128)(2,1)}, u32[]{:S(2)}) copy-start(bf16[2304,1152]{1,0:T(8,128)(2,1)} %param.11) | copy-start | bytes 15925252
Sparse Core Ops, SparseCore 0:
  73.3 128.9 all-reduce.1
where the time goes:
time: 218 us; the launch traced here: 217 us
  matrix products  121 us (56%)
  waiting for transfers between devices  57.2 us (26%)
  local copies, waits for them, and re-layouts  25.1 us (12%)
  between operations  14 us (6%)
    psum x1, waiting for transfers between devices, step(): dx = lax.psum(term.astype(jnp.bfloat16), 'tp')  57.2 us
    dot_general x1, matrix products, step(): d_hidden = jnp.dot(dy, w_down.T, preferred_element_type=jnp.float32)  26.2 us
    unnamed x5, local copies, waits for them, and re-layouts  25.1 us
    dot_general x1, matrix products, step(): jnp.dot(d_up, w_up.T, preferred_element_type=jnp.float32)  22.8 us
    dot_general x1, matrix products, step(): dw_up = jnp.dot(x.T, d_up, preferred_element_type=jnp.float32)  18.9 us
    dot_general x1, matrix products, step(): jnp.dot(hidden.astype(jnp.bfloat16).T, dy, preferred_element_type=jnp.flo...  18.8 us
    dot_general x1, matrix products, step(): dw_gate = jnp.dot(x.T, d_gate, preferred_element_type=jnp.float32)  17.1 us
    dot_general x1, matrix products, step(): jnp.dot(d_gate, w_gate.T, preferred_element_type=jnp.float32)  16.9 us
  transfers between devices with their start and end apart: 1, of which 1 were waited for; matrix products, arithmetic and copies ran while one was open for 33% of the time, Pallas kernels for 0%

commit v1 on v0

v1 whole, which is shorter than its diff:
```python
import functools

import jax
import jax.numpy as jnp
from jax import lax
from jax.experimental import pallas as pl
from jax.experimental.pallas import tpu as pltpu
from jax.sharding import PartitionSpec as P

ROWS, D, F = 2048, 2304, 1152
R = 256
H = R // 2
Q = D // 2
NK = ROWS // R
NC = 2 * NK
NT = (((1,), (1,)), ((), ()))
TN = (((0,), (0,)), ((), ()))
MESH = pl.DeviceIdType.MESH
f32, bf16 = jnp.float32, jnp.bfloat16
C1 = 0.7978845608028654
C3 = 0.044715

S_X, S_Y, S_END, DRAIN = 16, 25, 34, 6
AT = {
    2: (4, 4, 6, 6, 8, 8, 11, 11, 15, 15, 16, 16, 19, 19, 21, 21),
    3: (7, 7, 9, 9, 12, 12, 15, 15, 20, 20, 22, 22, 23, 23, 26, 26),
    4: (9, 10, 12, 13, 16, 17, 19, 20, 24, 24, 27, 27, 29, 29, 32, 32),
    5: (12, 15, 16, 18, 22, 22, 23, 23, 30, 31, 33, 34, 35, 36, 37, 38),
}


def act_back(g, u, d):
    g2 = g * g
    t = jnp.tanh(g * (C1 + (C1 * C3) * g2))
    cdf = 0.5 + 0.5 * t
    gelu = g * cdf
    slope = cdf + (0.5 * g) * (1.0 - t * t) * (C1 + (3 * C1 * C3) * g2)
    return gelu * u, d * u * slope, d * gelu


def main_kernel(
    x, dy, gate, up, wg, wu, wd,
    dx, wgu, wdo,
    gu, hid, dyv, gv, uv, xyv, term, psend, pin, r1, r2, kept1, kept2,
    ssem, rsem, wsem, isem, xsem,
):
    me = lax.axis_index("tp")
    xb, yb, cb = lax.div(me, 4), lax.rem(lax.div(me, 2), 2), lax.rem(me, 2)
    mate = me + 1 - 2 * cb

    weights = [
        pltpu.make_async_copy(wd, wdo, wsem.at[0]),
        pltpu.make_async_copy(wg, wgu.at[:, pl.ds(0, F)], wsem.at[1]),
        pltpu.make_async_copy(wu, wgu.at[:, pl.ds(F, F)], wsem.at[2]),
    ]

    def rows_in(k):
        slot = lax.rem(k, 2)
        rows = pl.ds(pl.multiple_of(k * R, R), R)
        return [
            pltpu.make_async_copy(src.at[rows], dst.at[slot], isem.at[i, slot])
            for i, (src, dst) in enumerate(((dy, dyv), (gate, gv), (up, uv)))
        ]

    def tile_in(src, j, q):
        slot = lax.rem(q, 2)
        columns = pl.ds(pl.multiple_of(j * 256, 256), 256)
        return pltpu.make_async_copy(src.at[:, columns], xyv.at[slot], xsem.at[slot])

    first = rows_in(0)
    first[0].start()
    weights[0].start()
    first[1].start()
    first[2].start()
    weights[1].start()
    weights[2].start()

    barrier = pltpu.get_barrier_semaphore()
    for other in (mate, me + 2 * (1 - 2 * yb), me + 4 * (1 - 2 * xb)):
        pl.semaphore_signal(barrier, inc=1, device_id={"tp": other}, device_id_type=MESH)
    pl.semaphore_wait(barrier, 3)

    def place(c):
        k, p = lax.div(c, 2), lax.rem(c, 2)
        b1 = xb * (1 - p) + yb * p
        b2 = yb * (1 - p) + xb * p
        n1 = me + (4 - 2 * p) * (1 - 2 * b1)
        n2 = me + (2 + 2 * p) * (1 - 2 * b2)
        return k, p, b1, b2, n1, n2

    def columns_of(p):
        return pl.ds(pl.multiple_of(p * Q, 128), Q)

    def remote(i, c, src, dst, to):
        return pltpu.make_async_remote_copy(
            src_ref=src, dst_ref=dst, send_sem=ssem.at[i, c], recv_sem=rsem.at[i, c],
            device_id={"tp": to}, device_id_type=MESH,
        )

    def sl(start, size, unit):
        return pl.ds(pl.multiple_of(start, unit), size)

    def mate_term(c):
        return remote(0, c, psend.at[lax.rem(c, 2)], pin.at[c], mate)

    def half_sum(c):
        k, p, b1, b2, n1, n2 = place(c)
        return remote(1, c, pin.at[c, sl(64 * (1 - b1), 64, 64)], r1.at[c], n1)

    def quarter_sum(c):
        k, p, b1, b2, n1, n2 = place(c)
        return remote(2, c, r1.at[c, sl(32 * (1 - b2), 32, 32)], r2.at[c], n2)

    def dx_copy(i, c, to, first_flip, second_flip, size):
        k, p, b1, b2, n1, n2 = place(c)
        r = k * R + cb * H + 64 * (b1 + first_flip * (1 - 2 * b1))
        if size == 32:
            r = r + 32 * (b2 + second_flip * (1 - 2 * b2))
        ref = dx.at[sl(r, size, 32), columns_of(p)]
        return remote(i, c, ref, ref, {"n1": n1, "n2": n2, "mate": mate}[to])

    def final(c, to):
        return dx_copy({"n2": 3, "n1": 4, "mate": 6}[to], c, to, 0, 0, 32)

    def forward(c, to):
        return dx_copy({"n1": 5, "mate": 7}[to], c, to, 0, 1, 32)

    def last(c):
        return dx_copy(8, c, "mate", 1, 0, 64)

    def blocks(n, body):
        lax.fori_loop(0, n, lambda i, z: (body(i), z)[1], 0)

    def stage0(k):
        for p in range(2):
            c = 2 * k + p

            @pl.when(k > 0)
            def _():
                mate_term(c - 2).wait_send()

            def body(i):
                rows = sl(H * (1 - cb) + 16 * i, 16, 16)
                psend[p, sl(16 * i, 16, 16), :] = term[rows, p * Q:(p + 1) * Q].astype(bf16)

            blocks(H // 16, body)
            mate_term(c).start()

    def stage1(c):
        k, p, b1, b2, n1, n2 = place(c)
        mate_term(c).wait_recv()
        cols = columns_of(p)

        def total(r):
            return term[sl(H * cb + r, 16, 16), cols] + pin[c, sl(r, 16, 16), :].astype(f32)

        def out(i):
            r = 64 * (1 - b1) + 16 * i
            pin[c, sl(r, 16, 16), :] = total(r).astype(bf16)

        def keep(i):
            kept1[lax.rem(c, 8), sl(16 * i, 16, 16), :] = total(64 * b1 + 16 * i)

        blocks(4, out)
        half_sum(c).start()
        blocks(4, keep)

    def stage2(c):
        k, p, b1, b2, n1, n2 = place(c)
        half_sum(c).wait_recv()

        def total(r):
            return kept1[lax.rem(c, 8), sl(r, 16, 16), :] + r1[c, sl(r, 16, 16), :].astype(f32)

        def out(i):
            r = 32 * (1 - b2) + 16 * i
            r1[c, sl(r, 16, 16), :] = total(r).astype(bf16)

        def keep(i):
            kept2[c, sl(16 * i, 16, 16), :] = total(32 * b2 + 16 * i)

        blocks(2, out)
        quarter_sum(c).start()
        blocks(2, keep)

    def stage3(c):
        k, p, b1, b2, n1, n2 = place(c)
        quarter_sum(c).wait_recv()
        base = k * R + cb * H + 64 * b1 + 32 * b2
        cols = columns_of(p)

        def body(i):
            t = kept2[c, sl(16 * i, 16, 16), :] + r2[c, sl(16 * i, 16, 16), :].astype(f32)
            dx[sl(base + 16 * i, 16, 16), cols] = t.astype(bf16)

        blocks(2, body)
        for to in ("n2", "n1", "mate"):
            final(c, to).start()

    def stage4(c):
        final(c, "n2").wait_recv()
        for to in ("n1", "mate"):
            forward(c, to).start()

    def stage5(c):
        final(c, "n1").wait_recv()
        forward(c, "n1").wait_recv()
        last(c).start()

    def count(stage, s):
        n = jnp.int32(0)
        for at in AT[stage]:
            n = n + jnp.where(s >= at, 1, 0)
        return n

    def serve(s):
        for stage, run in ((5, stage5), (4, stage4), (3, stage3), (2, stage2)):
            lax.fori_loop(
                count(stage, s - 1), count(stage, s), lambda c, z: (run(c), z)[1], 0
            )

    def chunk(k, z):
        slot = lax.rem(k, 2)

        @pl.when(k + 1 < NK)
        def _():
            for copy in rows_in(k + 1):
                copy.start()

        for copy in rows_in(k):
            copy.wait()

        @pl.when(k == 0)
        def _():
            weights[0].wait()

        rows = sl(k * R, R, R)
        for n0, n1 in ((0, 256), (256, 512), (512, 768), (768, 1024), (1024, 1152)):
            d = lax.dot_general(dyv[slot], wdo[n0:n1, :], NT, preferred_element_type=f32)
            h, dg, du = act_back(
                gv[slot, :, n0:n1].astype(f32), uv[slot, :, n0:n1].astype(f32), d
            )
            gu[rows, n0:n1] = dg.astype(bf16)
            gu[rows, F + n0:F + n1] = du.astype(bf16)
            hid[rows, n0:n1] = h.astype(bf16)

        @pl.when(k == 0)
        def _():
            weights[1].wait()
            weights[2].wait()

        @pl.when(k > 0)
        def _():
            stage1(2 * k - 2)
            stage1(2 * k - 1)

        serve(2 * k)
        for n0 in range(0, D, 768):
            term[:, n0:n0 + 768] = lax.dot_general(
                gu[rows, :], wgu[n0:n0 + 768, :], NT, preferred_element_type=f32
            )
        stage0(k)
        serve(2 * k + 1)
        return z

    lax.fori_loop(0, NK, chunk, 0)
    tile_in(x, 0, 0).start()
    lax.fori_loop(2 * NK - 2, 2 * NK, lambda c, z: (stage1(c), z)[1], 0)

    def x_tile(j, z):
        slot = lax.rem(j, 2)

        @pl.when(j + 1 < 9)
        def _():
            tile_in(x, j + 1, j + 1).start()

        @pl.when(j + 1 == 9)
        def _():
            tile_in(dy, 0, 9).start()

        tile_in(x, j, j).wait()
        rows = sl(j * 256, 256, 256)
        for n0 in range(0, D, 768):
            wgu[rows, n0:n0 + 768] = lax.dot_general(
                xyv[slot], gu[:, n0:n0 + 768], TN, preferred_element_type=f32
            ).astype(bf16)
        serve(S_X + j)
        return z

    lax.fori_loop(0, 9, x_tile, 0)

    def y_tile(j, z):
        slot = lax.rem(j + 1, 2)

        @pl.when(j + 1 < 9)
        def _():
            tile_in(dy, j + 1, j + 10).start()

        tile_in(dy, j, j + 9).wait()
        wdo[:, sl(j * 256, 256, 256)] = lax.dot_general(
            hid[...], xyv[slot], TN, preferred_element_type=f32
        ).astype(bf16)
        serve(S_Y + j)
        return z

    lax.fori_loop(0, 9, y_tile, 0)
    lax.fori_loop(S_END, S_END + DRAIN, lambda s, z: (serve(s), z)[1], 0)

    def finish(c, z):
        @pl.when(c >= NC - 2)
        def _():
            mate_term(c).wait_send()

        half_sum(c).wait_send()
        quarter_sum(c).wait_send()
        for to in ("n2", "n1", "mate"):
            final(c, to).wait_send()
        for to in ("n1", "mate"):
            forward(c, to).wait_send()
        last(c).wait_send()
        final(c, "mate").wait_recv()
        forward(c, "mate").wait_recv()
        last(c).wait_recv()
        return z

    lax.fori_loop(0, NC, finish, 0)


def write_kernel(dx, wgu, wdo, dx_o, wg_o, wu_o, wd_o, sem):
    copies = [
        pltpu.make_async_copy(dx, dx_o, sem.at[0]),
        pltpu.make_async_copy(wgu.at[:, pl.ds(0, F)], wg_o, sem.at[1]),
        pltpu.make_async_copy(wgu.at[:, pl.ds(F, F)], wu_o, sem.at[2]),
        pltpu.make_async_copy(wdo, wd_o, sem.at[3]),
    ]
    for copy in copies:
        copy.start()
    for copy in copies:
        copy.wait()


def solution(mesh):
    hbm = pl.BlockSpec(memory_space=pltpu.HBM)
    vmem = pl.BlockSpec(memory_space=pltpu.VMEM)

    def step(x, dy, gate, up, wg, wu, wd):
        dx, wgu, wdo = pl.pallas_call(
            main_kernel,
            name="mlp_back",
            out_shape=(
                pltpu.VMEM((ROWS, D), bf16),
                pltpu.VMEM((D, D), bf16),
                pltpu.VMEM((F, D), bf16),
            ),
            in_specs=[hbm] * 7,
            out_specs=(vmem,) * 3,
            scratch_shapes=[
                pltpu.VMEM((ROWS, D), bf16),
                pltpu.VMEM((ROWS, F), bf16),
                pltpu.VMEM((2, R, D), bf16),
                pltpu.VMEM((2, R, F), bf16),
                pltpu.VMEM((2, R, F), bf16),
                pltpu.VMEM((2, ROWS, 256), bf16),
                pltpu.VMEM((R, D), f32),
                pltpu.VMEM((2, H, Q), bf16),
                pltpu.VMEM((NC, H, Q), bf16),
                pltpu.VMEM((NC, 64, Q), bf16),
                pltpu.VMEM((NC, 32, Q), bf16),
                pltpu.VMEM((8, 64, Q), f32),
                pltpu.VMEM((NC, 32, Q), f32),
                pltpu.SemaphoreType.DMA((9, NC)),
                pltpu.SemaphoreType.DMA((9, NC)),
                pltpu.SemaphoreType.DMA((3,)),
                pltpu.SemaphoreType.DMA((3, 2)),
                pltpu.SemaphoreType.DMA((2,)),
            ],
            compiler_params=pltpu.CompilerParams(
                collective_id=0, has_side_effects=True, vmem_limit_bytes=39 * 2**20
            ),
            cost_estimate=pl.CostEstimate(
                flops=12 * ROWS * D * F, bytes_accessed=80 * 2**20, transcendentals=ROWS * F
            ),
        )(x, dy, gate, up, wg, wu, wd)
        return pl.pallas_call(
            write_kernel,
            name="write_out",
            out_shape=(
                jax.ShapeDtypeStruct((ROWS, D), bf16),
                jax.ShapeDtypeStruct((D, F), bf16),
                jax.ShapeDtypeStruct((D, F), bf16),
                jax.ShapeDtypeStruct((F, D), bf16),
            ),
            in_specs=[vmem] * 3,
            out_specs=(hbm,) * 4,
            scratch_shapes=[pltpu.SemaphoreType.DMA((4,))],
            compiler_params=pltpu.CompilerParams(vmem_limit_bytes=8 * 2**20),
        )(dx, wgu, wdo)

    tokens, columns, rows = P("dp", None), P(None, "tp"), P("tp", None)
    return jax.shard_map(
        step,
        mesh=mesh,
        in_specs=(tokens, tokens, P("dp", "tp"), P("dp", "tp"), columns, columns, rows),
        out_specs=(tokens, P("dp", "tp"), P("dp", "tp"), P(("dp", "tp"), None)),
        check_vma=False,
    )
```

time: 218 us -> 114 us (0.52)
  matrix products: 121 us -> 0 us
  Pallas kernels: 0 us -> 113 us
  waiting for transfers between devices: 57.2 us -> 0 us
  local copies, waits for them, and re-layouts: 25.1 us -> 0 us
  between operations: 14 us -> 0.64 us
    dot_general x6 -> x0, matrix products: 121 us -> none  [the longest x1 26.2 us: step(): d_hidden = jnp.dot(dy, w_down.T, preferred_element_type=jnp.float32)]
    pallas_call x0 -> x2, Pallas kernels: none -> 113 us  [the longest x1 105 us: step(): pl.pallas_call(main_kernel, name='mlp_back', out_shape=(pltpu.VMEM((ROWS,...]
    psum x1 -> x0, waiting for transfers between devices: 57.2 us -> none  [step(): dx = lax.psum(term.astype(jnp.bfloat16), 'tp')]
    unnamed x5 -> x0, local copies, waits for them, and re-layouts: 25.1 us -> none
  transfers between devices with their start and end apart: 1 -> 0, of which waited for: 1 -> 0; matrix products, arithmetic and copies ran while one was open for 33% -> 0% of each run, Pallas kernels for 0% -> 0%
where the time goes in v1:
time: 114 us
  Pallas kernels  113 us (99%)
    pallas_call x1, Pallas kernels, step(): pl.pallas_call(main_kernel, name='mlp_back', out_shape=(pltpu.VMEM((ROWS,...  105 us
    pallas_call x1, Pallas kernels, step(): pl.pallas_call(write_kernel, name='write_out', out_shape=(jax.ShapeDtypeS...  8.72 us

profile of v1, /device:TPU:0, one launch (start us, length us, event | category | flops | bytes accessed | tf_op | source)
XLA Modules:
  0.0 114.0 jit_solution(3609327178335301485)
XLA Ops:
  0.6 104.6 %mlp_back.1 = (bf16[2048,2304]{1,0:T(8,128)(2,1)S(1)}, bf16[2304,2304]{1,0:T(8,128)(2,1)S(1)}, bf16[1152,2304]{1,0:T(8,128)(2,1)S(1)}) custom-call(bf16[2048,2304]{1,0:T(8,128)(2,1)} %x.1, bf16[2048,2304]{1,0:T(8,128)(2,1)} %dy.1, bf16[2048,1152]{1,0:T(8,128)(2,1)} %gate.1, bf16[2048,1152]{1,0:T(8,128)(2,1)} %up.1, bf16[2304,1152]{1,0:T(8,128)(2,1)} %wg.1, ...), custom_call_target="tpu_custom_call" | custom-call | flops 65229815808 | bytes 83886080 | tf_op jit(solution)/shard_map/mlp_back/pallas_call | solution.py:347
  105.3 8.7 %write_out.1 = (bf16[2048,2304]{1,0:T(8,128)(2,1)}, bf16[2304,1152]{1,0:T(8,128)(2,1)}, bf16[2304,1152]{1,0:T(8,128)(2,1)}, bf16[1152,2304]{1,0:T(8,128)(2,1)}) custom-call(bf16[2048,2304]{1,0:T(8,128)(2,1)S(1)} %get-tuple-element.7.dx, bf16[2304,2304]{1,0:T(8,128)(2,1)S(1)} %get-tuple-element.8.wgu, bf16[1152,2304]{1,0:T(8,128)(2,1)S(1)} %get-tuple-element.9.wdo), custom_call_target="tpu_custom_call" | custom-call | tf_op jit(solution)/shard_map/write_out/pallas_call | solution.py:384

commit v2 on v0

v2 whole, which is shorter than its diff:
```python
import functools

import jax
import jax.numpy as jnp
from jax import lax
from jax.experimental import pallas as pl
from jax.experimental.pallas import tpu as pltpu
from jax.sharding import PartitionSpec as P

ROWS, D, F = 2048, 2304, 1152
R = 256
H = R // 2
Q = D // 2
NK = ROWS // R
NT = (((1,), (1,)), ((), ()))
TN = (((0,), (0,)), ((), ()))
MESH = pl.DeviceIdType.MESH
f32, bf16 = jnp.float32, jnp.bfloat16
C1 = 0.7978845608028654
C3 = 0.044715

S_X, S_Y, S_END = 14, 23, 32
AT = {
    2: (3, 4, 6, 9, 11, 13, 17, 19),
    3: (5, 7, 10, 13, 15, 19, 21, 23),
    4: (8, 14, 21, 21, 22, 25, 27, 29),
    5: (17, 19, 27, 29, 30, 32, 33, 34),
}
EARLY, EARLY_CHUNKS = 33, 6
D_TILES = ((0, 256), (256, 512), (512, 768), (768, 1024), (1024, 1152))


def act_back(g, u, d):
    g2 = g * g
    t = jnp.tanh(g * (C1 + (C1 * C3) * g2))
    cdf = 0.5 + 0.5 * t
    gelu = g * cdf
    slope = cdf + (0.5 * g) * (1.0 - t * t) * (C1 + (3 * C1 * C3) * g2)
    return gelu * u, d * u * slope, d * gelu


def main_kernel(
    x, dy, gate, up, wg, wu, wd,
    dx, wgu, wdo,
    gu, hid, cur0, cur1, dyv, gv, uv, xyv, own, psend, pin, r1, r2, kept1, kept2,
    ssem, rsem, wsem, isem, xsem,
):
    me = lax.axis_index("tp")
    xb, yb, cb = lax.div(me, 4), lax.rem(lax.div(me, 2), 2), lax.rem(me, 2)
    mate = me + 1 - 2 * cb

    def wd_in(i):
        rows = pl.ds((0, 512)[i], (512, 640)[i])
        return pltpu.make_async_copy(wd.at[rows], wdo.at[rows], wsem.at[0, i])

    def wgu_in(i):
        rows = pl.ds(768 * i, 768)
        return [
            pltpu.make_async_copy(w.at[rows], wgu.at[rows, pl.ds(F * q, F)], wsem.at[1 + q, i])
            for q, w in enumerate((wg, wu))
        ]

    def half_rows(k, half):
        at = k * R + H * (half * cb + (1 - half) * (1 - cb))
        return pl.ds(pl.multiple_of(at, H), H)

    def rows_in(k):
        slot = lax.rem(k, 2)
        return [
            pltpu.make_async_copy(
                src.at[half_rows(k, half)],
                dst.at[slot, pl.ds(H * half, H)],
                isem.at[i, half, slot],
            )
            for i, (src, dst) in enumerate(((dy, dyv), (gate, gv), (up, uv)))
            for half in range(2)
        ]

    def tile_in(src, j, q):
        slot = lax.rem(q, 2)
        columns = pl.ds(pl.multiple_of(j * 256, 256), 256)
        return pltpu.make_async_copy(src.at[:, columns], xyv.at[slot], xsem.at[slot])

    for copy in rows_in(0):
        copy.start()
    for i in range(2):
        wd_in(i).start()

    barrier = pltpu.get_barrier_semaphore()
    for other in (mate, me + 2 * (1 - 2 * yb), me + 4 * (1 - 2 * xb)):
        pl.semaphore_signal(barrier, inc=1, device_id={"tp": other}, device_id_type=MESH)

    x_pair, y_pair = (xb, me + 4 * (1 - 2 * xb)), (yb, me + 2 * (1 - 2 * yb))
    LINKS = ((x_pair, y_pair), (y_pair, x_pair))

    def remote(i, k, p, src, dst, to):
        return pltpu.make_async_remote_copy(
            src_ref=src, dst_ref=dst, send_sem=ssem.at[i, p, k], recv_sem=rsem.at[i, p, k],
            device_id={"tp": to}, device_id_type=MESH,
        )

    def sl(start, size, unit):
        return pl.ds(pl.multiple_of(start, unit), size)

    keep1, give1, keep2, give2 = ([f(p) for p in range(2)] for f in (
        lambda p: 64 * LINKS[p][0][0],
        lambda p: 64 - 64 * LINKS[p][0][0],
        lambda p: 32 * LINKS[p][1][0],
        lambda p: 32 - 32 * LINKS[p][1][0],
    ))

    def mate_term(k, p):
        return remote(0, k, p, psend.at[p], pin.at[p, k], mate)

    def half_sum(k, p):
        return remote(1, k, p, pin.at[p, k, sl(give1[p], 64, 64)], r1.at[p, k], LINKS[p][0][1])

    def quarter_sum(k, p):
        return remote(2, k, p, r1.at[p, k, sl(give2[p], 32, 32)], r2.at[p, k], LINKS[p][1][1])

    def dx_copy(i, k, p, to, row, size):
        ref = dx.at[sl(k * R + (cb * H + row), size, 32), p * Q:(p + 1) * Q]
        return remote(i, k, p, ref, ref, to)

    def final(k, p, to):
        i, device = {
            "second": (3, LINKS[p][1][1]), "first": (4, LINKS[p][0][1]), "mate": (6, mate)
        }[to]
        return dx_copy(i, k, p, device, keep1[p] + keep2[p], 32)

    def forward(k, p, to):
        i, device = {"first": (5, LINKS[p][0][1]), "mate": (7, mate)}[to]
        return dx_copy(i, k, p, device, keep1[p] + give2[p], 32)

    def last(k, p):
        return dx_copy(8, k, p, mate, give1[p], 64)

    def ring(k):
        return lax.rem(k, 4)

    def stage1(k, p):
        mate_term(k, p).wait_recv()

        def total(r):
            mine = own[sl(r, 16, 16), p * Q:(p + 1) * Q]
            return mine + pin[p, k, sl(r, 16, 16), :].astype(f32)

        for i in range(4):
            r = give1[p] + 16 * i
            pin[p, k, sl(r, 16, 16), :] = total(r).astype(bf16)
        half_sum(k, p).start()
        for i in range(4):
            kept1[p, ring(k), 16 * i:16 * i + 16, :] = total(keep1[p] + 16 * i)

    def stage2(k, p):
        half_sum(k, p).wait_recv()

        def total(r):
            mine = kept1[p, ring(k), sl(r, 16, 16), :]
            return mine + r1[p, k, sl(r, 16, 16), :].astype(f32)

        for i in range(2):
            r = give2[p] + 16 * i
            r1[p, k, sl(r, 16, 16), :] = total(r).astype(bf16)
        quarter_sum(k, p).start()
        for i in range(2):
            kept2[p, ring(k), 16 * i:16 * i + 16, :] = total(keep2[p] + 16 * i)

    def stage3(k, p):
        quarter_sum(k, p).wait_recv()
        base = k * R + (cb * H + keep1[p] + keep2[p])
        for i in range(2):
            part = slice(16 * i, 16 * i + 16)
            t = kept2[p, ring(k), part, :] + r2[p, k, part, :].astype(f32)
            dx[sl(base + 16 * i, 16, 16), p * Q:(p + 1) * Q] = t.astype(bf16)
        for to in ("second", "first", "mate"):
            final(k, p, to).start()

    def stage4(k, p):
        final(k, p, "second").wait_recv()
        for to in ("first", "mate"):
            forward(k, p, to).start()

    def stage5(k, p):
        final(k, p, "first").wait_recv()
        forward(k, p, "first").wait_recv()
        last(k, p).start()

    STAGES = {2: stage2, 3: stage3, 4: stage4, 5: stage5}

    def run_step(step):
        for stage in (5, 4, 3, 2):
            for k in range(NK):
                if AT[stage][k] == step:
                    STAGES[stage](k, 0)
                    STAGES[stage](k, 1)

    def serve(i, first, stride, turns):
        for v in range(turns):
            if any(first + stride * v in at for at in AT.values()):
                pl.when(i == v)(functools.partial(run_step, first + stride * v))

    def back_tile(k, cur, n0, n1):
        slot = lax.rem(k, 2)
        d = lax.dot_general(dyv[slot], wdo[n0:n1, :], NT, preferred_element_type=f32)
        grads = act_back(gv[slot, :, n0:n1].astype(f32), uv[slot, :, n0:n1].astype(f32), d)
        h, dg, du = (g.astype(bf16) for g in grads)
        cur[:, n0:n1] = dg
        cur[:, F + n0:F + n1] = du
        for half in range(2):
            rows, part = half_rows(k, half), slice(H * half, H * half + H)
            gu[rows, n0:n1] = dg[part]
            gu[rows, F + n0:F + n1] = du[part]
            hid[rows, n0:n1] = h[part]

    def term_tile(cur, n0):
        t = lax.dot_general(
            cur[...], wgu[n0:n0 + 768, :], NT, preferred_element_type=f32
        )
        own[:, n0:n0 + 768] = t[H:]
        for p, q0, q1 in ((0, n0, min(n0 + 768, Q)), (1, max(n0, Q), n0 + 768)):
            if q0 < q1:
                psend[p, :, q0 - p * Q:q1 - p * Q] = t[:H, q0 - n0:q1 - n0].astype(bf16)

    def send_term(k):
        for p in range(2):
            mate_term(k, p).start()

    def chunk_sum(k):
        stage1(k, 0)
        stage1(k, 1)

    def chunk_step(m, k, first, cur, ahead, start_rows):
        for p in range(2):
            mate_term(k - 1, p).wait_send()
        for copy in rows_in(k + 1):
            copy.wait()
        start_rows()
        for n0 in range(0, D, 768):
            term_tile(cur, n0)
        send_term(k)
        serve(m, first, 4, 3)
        for n0, n1 in D_TILES:
            back_tile(k + 1, ahead, n0, n1)
        chunk_sum(k)
        serve(m, first + 1, 4, 3)

    for copy in rows_in(0):
        copy.wait()
    for i in range(3):
        for copy in wgu_in(i):
            copy.start()
    wd_in(0).wait()
    for n0, n1 in D_TILES:
        if n0 == 512:
            wd_in(1).wait()
        back_tile(0, cur0, n0, n1)
    for copy in rows_in(1):
        copy.start()
    for i in range(3):
        for copy in wgu_in(i):
            copy.wait()
        term_tile(cur0, 768 * i)
    pl.semaphore_wait(barrier, 3)
    send_term(0)
    for copy in rows_in(1):
        copy.wait()
    for copy in rows_in(2):
        copy.start()
    for n0, n1 in D_TILES:
        back_tile(1, cur1, n0, n1)
    chunk_sum(0)

    def two_chunks(m, z):
        def next_rows(k):
            for copy in rows_in(k):
                copy.start()

        chunk_step(m, 2 * m + 1, 1, cur1, cur0, lambda: next_rows(2 * m + 3))
        chunk_step(
            m, 2 * m + 2, 3, cur0, cur1,
            lambda: pl.when(m < 2)(lambda: next_rows(2 * m + 4)),
        )
        return z

    lax.fori_loop(0, NK // 2 - 1, two_chunks, 0)
    tile_in(x, 0, 0).start()
    for p in range(2):
        mate_term(NK - 2, p).wait_send()
    for n0 in range(0, D, 768):
        term_tile(cur1, n0)
    send_term(NK - 1)
    run_step(2 * NK - 3)

    def x_tile(j, z):
        slot = lax.rem(j, 2)

        @pl.when(j + 1 < 9)
        def _():
            tile_in(x, j + 1, j + 1).start()

        @pl.when(j + 1 == 9)
        def _():
            tile_in(dy, 0, 9).start()

        tile_in(x, j, j).wait()
        rows = sl(j * 256, 256, 256)
        for n0 in range(0, D, 768):
            wgu[rows, n0:n0 + 768] = lax.dot_general(
                xyv[slot], gu[:, n0:n0 + 768], TN, preferred_element_type=f32
            ).astype(bf16)

        @pl.when(j == 0)
        def _():
            chunk_sum(NK - 1)

        serve(j, S_X, 1, 9)
        return z

    lax.fori_loop(0, 9, x_tile, 0)

    def y_tile(j, z):
        slot = lax.rem(j + 1, 2)

        @pl.when(j + 1 < 9)
        def _():
            tile_in(dy, j + 1, j + 10).start()

        tile_in(dy, j, j + 9).wait()
        wdo[:, sl(j * 256, 256, 256)] = lax.dot_general(
            hid[...], xyv[slot], TN, preferred_element_type=f32
        ).astype(bf16)
        serve(j, S_Y, 1, 9)
        return z

    lax.fori_loop(0, 9, y_tile, 0)
    def finish(k):
        for p in range(2):
            half_sum(k, p).wait_send()
            quarter_sum(k, p).wait_send()
            for to in ("second", "first", "mate"):
                final(k, p, to).wait_send()
            for to in ("first", "mate"):
                forward(k, p, to).wait_send()
            last(k, p).wait_send()
            final(k, p, "mate").wait_recv()
            forward(k, p, "mate").wait_recv()
            last(k, p).wait_recv()

    for p in range(2):
        mate_term(NK - 1, p).wait_send()
    for step in range(S_END, max(AT[5]) + 1):
        run_step(step)
        if step == EARLY:
            for k in range(EARLY_CHUNKS):
                finish(k)
    for k in range(EARLY_CHUNKS, NK):
        finish(k)


def write_kernel(dx, wgu, wdo, dx_o, wg_o, wu_o, wd_o, sem):
    copies = [
        pltpu.make_async_copy(dx, dx_o, sem.at[0]),
        pltpu.make_async_copy(wgu.at[:, pl.ds(0, F)], wg_o, sem.at[1]),
        pltpu.make_async_copy(wgu.at[:, pl.ds(F, F)], wu_o, sem.at[2]),
        pltpu.make_async_copy(wdo, wd_o, sem.at[3]),
    ]
    for copy in copies:
        copy.start()
    for copy in copies:
        copy.wait()


def solution(mesh):
    hbm = pl.BlockSpec(memory_space=pltpu.HBM)
    vmem = pl.BlockSpec(memory_space=pltpu.VMEM)

    def step(x, dy, gate, up, wg, wu, wd):
        results = pl.pallas_call(
            main_kernel,
            name="mlp_back",
            out_shape=(
                pltpu.VMEM((ROWS, D), bf16),
                pltpu.VMEM((D, D), bf16),
                pltpu.VMEM((F, D), bf16),
            ),
            in_specs=[hbm] * 7,
            out_specs=(vmem,) * 3,
            scratch_shapes=[
                pltpu.VMEM((ROWS, D), bf16),
                pltpu.VMEM((ROWS, F), bf16),
                pltpu.VMEM((R, D), bf16),
                pltpu.VMEM((R, D), bf16),
                pltpu.VMEM((2, R, D), bf16),
                pltpu.VMEM((2, R, F), bf16),
                pltpu.VMEM((2, R, F), bf16),
                pltpu.VMEM((2, ROWS, 256), bf16),
                pltpu.VMEM((H, D), f32),
                pltpu.VMEM((2, H, Q), bf16),
                pltpu.VMEM((2, NK, H, Q), bf16),
                pltpu.VMEM((2, NK, 64, Q), bf16),
                pltpu.VMEM((2, NK, 32, Q), bf16),
                pltpu.VMEM((2, 4, 64, Q), f32),
                pltpu.VMEM((2, 4, 32, Q), f32),
                pltpu.SemaphoreType.DMA((9, 2, NK)),
                pltpu.SemaphoreType.DMA((9, 2, NK)),
                pltpu.SemaphoreType.DMA((3, 3)),
                pltpu.SemaphoreType.DMA((3, 2, 2)),
                pltpu.SemaphoreType.DMA((2,)),
            ],
            compiler_params=pltpu.CompilerParams(
                collective_id=0, has_side_effects=True, vmem_limit_bytes=38 * 2**20
            ),
            cost_estimate=pl.CostEstimate(
                flops=12 * ROWS * D * F, bytes_accessed=80 * 2**20, transcendentals=ROWS * F
            ),
        )(x, dy, gate, up, wg, wu, wd)
        return pl.pallas_call(
            write_kernel,
            name="write_out",
            out_shape=(
                jax.ShapeDtypeStruct((ROWS, D), bf16),
                jax.ShapeDtypeStruct((D, F), bf16),
                jax.ShapeDtypeStruct((D, F), bf16),
                jax.ShapeDtypeStruct((F, D), bf16),
            ),
            in_specs=[vmem] * 3,
            out_specs=(hbm,) * 4,
            scratch_shapes=[pltpu.SemaphoreType.DMA((4,))],
            compiler_params=pltpu.CompilerParams(vmem_limit_bytes=8 * 2**20),
        )(*results)

    tokens, columns, rows = P("dp", None), P(None, "tp"), P("tp", None)
    return jax.shard_map(
        step,
        mesh=mesh,
        in_specs=(tokens, tokens, P("dp", "tp"), P("dp", "tp"), columns, columns, rows),
        out_specs=(tokens, P("dp", "tp"), P("dp", "tp"), P(("dp", "tp"), None)),
        check_vma=False,
    )
```

time: 218 us -> 110 us (0.50)
  matrix products: 121 us -> 0 us
  Pallas kernels: 0 us -> 109 us
  waiting for transfers between devices: 57.2 us -> 0 us
  local copies, waits for them, and re-layouts: 25.1 us -> 0 us
  between operations: 14 us -> 0.82 us
    dot_general x6 -> x0, matrix products: 121 us -> none  [the longest x1 26.2 us: step(): d_hidden = jnp.dot(dy, w_down.T, preferred_element_type=jnp.float32)]
    pallas_call x0 -> x2, Pallas kernels: none -> 109 us  [the longest x1 100 us: step(): pl.pallas_call(main_kernel, name='mlp_back', out_shape=(pltpu.VMEM((ROWS,...]
    psum x1 -> x0, waiting for transfers between devices: 57.2 us -> none  [step(): dx = lax.psum(term.astype(jnp.bfloat16), 'tp')]
    unnamed x5 -> x0, local copies, waits for them, and re-layouts: 25.1 us -> none
  transfers between devices with their start and end apart: 1 -> 0, of which waited for: 1 -> 0; matrix products, arithmetic and copies ran while one was open for 33% -> 0% of each run, Pallas kernels for 0% -> 0%
where the time goes in v2:
time: 110 us
  Pallas kernels  109 us (99%)
    pallas_call x1, Pallas kernels, step(): pl.pallas_call(main_kernel, name='mlp_back', out_shape=(pltpu.VMEM((ROWS,...  100 us
    pallas_call x1, Pallas kernels, step(): pl.pallas_call(write_kernel, name='write_out', out_shape=(jax.ShapeDtypeS...  8.72 us

profile of v2, /device:TPU:0, one launch (start us, length us, event | category | flops | bytes accessed | tf_op | source)
XLA Modules:
  0.0 109.6 jit_solution(8794406979116714770)
XLA Ops:
  0.6 100.1 %mlp_back.1 = (bf16[2048,2304]{1,0:T(8,128)(2,1)S(1)}, bf16[2304,2304]{1,0:T(8,128)(2,1)S(1)}, bf16[1152,2304]{1,0:T(8,128)(2,1)S(1)}) custom-call(bf16[2048,2304]{1,0:T(8,128)(2,1)} %x.1, bf16[2048,2304]{1,0:T(8,128)(2,1)} %dy.1, bf16[2048,1152]{1,0:T(8,128)(2,1)} %gate.1, bf16[2048,1152]{1,0:T(8,128)(2,1)} %up.1, bf16[2304,1152]{1,0:T(8,128)(2,1)} %wg.1, ...), custom_call_target="tpu_custom_call" | custom-call | flops 65229815808 | bytes 83886080 | tf_op jit(solution)/shard_map/mlp_back/pallas_call | solution.py:379
  100.7 8.7 %write_out.1 = (bf16[2048,2304]{1,0:T(8,128)(2,1)}, bf16[2304,1152]{1,0:T(8,128)(2,1)}, bf16[2304,1152]{1,0:T(8,128)(2,1)}, bf16[1152,2304]{1,0:T(8,128)(2,1)}) custom-call(bf16[2048,2304]{1,0:T(8,128)(2,1)S(1)} %get-tuple-element.7.dx, bf16[2304,2304]{1,0:T(8,128)(2,1)S(1)} %get-tuple-element.8.wgu, bf16[1152,2304]{1,0:T(8,128)(2,1)S(1)} %get-tuple-element.9.wdo), custom_call_target="tpu_custom_call" | custom-call | tf_op jit(solution)/shard_map/write_out/pallas_call | solution.py:418

commit v3 on v2

--- a/solution.py
+++ b/solution.py
@@ -21,12 +21,12 @@
 
 S_X, S_Y, S_END = 14, 23, 32
 AT = {
-    2: (3, 4, 6, 9, 11, 13, 17, 19),
-    3: (5, 7, 10, 13, 15, 19, 21, 23),
-    4: (8, 14, 21, 21, 22, 25, 27, 29),
-    5: (17, 19, 27, 29, 30, 32, 33, 34),
+    2: (3, 4, 9, 9, 12, 17, 19, 19),
+    3: (5, 6, 13, 14, 19, 20, 22, 24),
+    4: (8, 15, 16, 18, 25, 25, 28, 29),
+    5: (13, 24, 25, 26, 29, 30, 32, 33),
 }
-EARLY, EARLY_CHUNKS = 33, 6
+EARLY, EARLY_CHUNKS = 32, 6
 D_TILES = ((0, 256), (256, 512), (512, 768), (768, 1024), (1024, 1152))
 
 
@@ -349,7 +349,7 @@
 
     for p in range(2):
         mate_term(NK - 1, p).wait_send()
-    for step in range(S_END, max(AT[5]) + 1):
+    for step in range(S_END, max(*AT[5], EARLY) + 1):
         run_step(step)
         if step == EARLY:
             for k in range(EARLY_CHUNKS):
@@ -359,12 +359,16 @@
 
 
 def write_kernel(dx, wgu, wdo, dx_o, wg_o, wu_o, wd_o, sem):
-    copies = [
-        pltpu.make_async_copy(dx, dx_o, sem.at[0]),
-        pltpu.make_async_copy(wgu.at[:, pl.ds(0, F)], wg_o, sem.at[1]),
-        pltpu.make_async_copy(wgu.at[:, pl.ds(F, F)], wu_o, sem.at[2]),
-        pltpu.make_async_copy(wdo, wd_o, sem.at[3]),
-    ]
+    copies = []
+    for at in range(4):
+        for src, dst in (
+            (dx, dx_o), (wgu.at[:, pl.ds(0, F)], wg_o), (wgu.at[:, pl.ds(F, F)], wu_o), (wdo, wd_o)
+        ):
+            size = src.shape[0] // 4
+            rows = pl.ds(at * size, size)
+            copies.append(
+                pltpu.make_async_copy(src.at[rows], dst.at[rows], sem.at[len(copies)])
+            )
     for copy in copies:
         copy.start()
     for copy in copies:
@@ -426,7 +430,7 @@
             ),
             in_specs=[vmem] * 3,
             out_specs=(hbm,) * 4,
-            scratch_shapes=[pltpu.SemaphoreType.DMA((4,))],
+            scratch_shapes=[pltpu.SemaphoreType.DMA((16,))],
             compiler_params=pltpu.CompilerParams(vmem_limit_bytes=8 * 2**20),
         )(*results)
 

time: 110 us -> 109 us (level)
  no operation moved by 1% of the time
where the time goes in v3:
time: 109 us
  Pallas kernels  108 us (99%)
    pallas_call x1, Pallas kernels, step(): pl.pallas_call(main_kernel, name='mlp_back', out_shape=(pltpu.VMEM((ROWS,...  99.5 us
    pallas_call x1, Pallas kernels, step(): pl.pallas_call(write_kernel, name='write_out', out_shape=(jax.ShapeDtypeS...  8.58 us

profile of v3, /device:TPU:0, one launch (start us, length us, event | category | flops | bytes accessed | tf_op | source)
XLA Modules:
  0.0 108.9 jit_solution(8880653205441575623)
XLA Ops:
  0.6 99.5 %mlp_back.1 = (bf16[2048,2304]{1,0:T(8,128)(2,1)S(1)}, bf16[2304,2304]{1,0:T(8,128)(2,1)S(1)}, bf16[1152,2304]{1,0:T(8,128)(2,1)S(1)}) custom-call(bf16[2048,2304]{1,0:T(8,128)(2,1)} %x.1, bf16[2048,2304]{1,0:T(8,128)(2,1)} %dy.1, bf16[2048,1152]{1,0:T(8,128)(2,1)} %gate.1, bf16[2048,1152]{1,0:T(8,128)(2,1)} %up.1, bf16[2304,1152]{1,0:T(8,128)(2,1)} %wg.1, ...), custom_call_target="tpu_custom_call" | custom-call | flops 65229815808 | bytes 83886080 | tf_op jit(solution)/shard_map/mlp_back/pallas_call | solution.py:383
  100.2 8.6 %write_out.1 = (bf16[2048,2304]{1,0:T(8,128)(2,1)}, bf16[2304,1152]{1,0:T(8,128)(2,1)}, bf16[2304,1152]{1,0:T(8,128)(2,1)}, bf16[1152,2304]{1,0:T(8,128)(2,1)}) custom-call(bf16[2048,2304]{1,0:T(8,128)(2,1)S(1)} %get-tuple-element.7.dx, bf16[2304,2304]{1,0:T(8,128)(2,1)S(1)} %get-tuple-element.8.wgu, bf16[1152,2304]{1,0:T(8,128)(2,1)S(1)} %get-tuple-element.9.wdo), custom_call_target="tpu_custom_call" | custom-call | tf_op jit(solution)/shard_map/write_out/pallas_call | solution.py:422
